TPU v7x, 128 devices: a whole 4x4x4 slice. The times are simulated.
128 devices in a mesh: rep: 1, sub: 16 (over z, y), blk: 8 (over x, core).
Axes of the slice: x: 4, y: 4, z: 4, core: 2. Of those that a mesh axis runs over, the one named last changes fastest.
Arguments:
- ratings: float32 [262144, 512], P(('rep', 'blk', 'sub'))
- mask: int32 [262144, 512], P(('rep', 'blk', 'sub'))
- user_init: float32 [262144, 32], P(('rep', 'blk', 'sub'))
- item_init: float32 [512, 32], P(('rep', 'blk'))
Outputs:
- output 1: float32 [262144, 32], P(('rep', 'blk', 'sub'))
- output 2: float32 [512, 32], P(('rep', 'blk'))
All inputs are finite; a program needn't handle non-finite values.
Results may differ from a plain program's by a relative error of at most 0.001.
Values are sent between devices in bfloat16 or wider.
A program may use at most 1 GiB of HBM per device.

v0:
```python
import math
import jax
import jax.numpy as jnp
from jax import lax
from jax.sharding import PartitionSpec as P

STEPS = 4
EPOCHS = 2
STEP_GAIN = 0.4
DECAY = 0.002


def solution(mesh):
    blk_size = mesh.shape['blk']
    sub_size = mesh.shape['sub']
    row_spec = P(('rep', 'blk', 'sub'), None)
    item_spec = P(('rep', 'blk'), None)
    prev_pairs = [(source_idx, (source_idx - 1) % blk_size) for source_idx in range(blk_size)]

    def local_run(ratings, mask, user_init, item_init):
        users_dev = ratings.shape[0]
        items_dev, factor_dim = item_init.shape
        big_side = max(items_dev, sub_size * users_dev)
        step_size = STEP_GAIN * math.sqrt(factor_dim) / (math.sqrt(big_side) + math.sqrt(factor_dim)) ** 2
        decay_coef = DECAY / step_size
        blk_pos = lax.axis_index('blk')

        def sub_epoch(counter, state):
            user_st, item_st = state
            col_start = ((blk_pos + counter) % blk_size) * items_dev
            rating_now = lax.dynamic_slice_in_dim(ratings, col_start, items_dev, axis=1)
            mask_now = lax.dynamic_slice_in_dim(mask, col_start, items_dev, axis=1) != 0
            for step_idx in range(STEPS):
                user_half = user_st.astype(jnp.bfloat16)
                item_half = item_st.astype(jnp.bfloat16)
                predicted = lax.dot_general(user_half, item_half, (((1,), (1,)), ((), ())), preferred_element_type=jnp.float32)
                err_half = jnp.where(mask_now, predicted - rating_now, 0.0).astype(jnp.bfloat16)
                grad_user = jnp.dot(err_half, item_half, preferred_element_type=jnp.float32) + decay_coef * user_st
                part_item = lax.dot_general(err_half, user_half, (((0,), (0,)), ((), ())), preferred_element_type=jnp.float32)
                grad_item = lax.psum(part_item, 'sub') + decay_coef * item_st
                user_st = user_st - step_size * grad_user
                item_st = item_st - step_size * grad_item
            return user_st, lax.ppermute(item_st, 'blk', prev_pairs)

        return lax.fori_loop(0, EPOCHS * blk_size, sub_epoch, (user_init, item_init))

    return jax.shard_map(local_run, mesh=mesh, in_specs=(row_spec, row_spec, row_spec, item_spec), out_specs=(row_spec, item_spec), check_vma=False)
```

profile of v0, /device:TPU:1, one launch (start us, length us, event | category | flops | bytes accessed | tf_op | source)
XLA Modules:
  0.0 4619.9 jit_solution(18077577888270657164)
XLA Ops:
  11.5 4607.8 %while.17 = (s32[]{:T(128)}, f32[2048,32]{0,1:T(8,128)S(1)}, f32[64,32]{0,1:T(8,128)S(1)}, s32[]{:T(128)}, s32[2048,512]{0,1:T(8,128)}, /*index=5*/f32[2048,512]...) while((s32[]{:T(128)}, f32[2048,32]{0,1:T(8,128)S(1)}, ...), condition=%wide.region_5.6_spmd, body=%wide.region_0.5_spmd.sunk | while | flops 104009744 | bytes 10903896 | solution.py:45
  14.3 62.5 %psum.60 = f32[64,32]{0,1:T(8,128)S(1)} all-reduce(f32[64,32]{0,1:T(8,128)S(1)} %fusion.110), channel_id=1, replica_groups=mesh['rep'=1,'sub'=16,'blk'=8] {'sub'}, use_global_device_ids=true, to_apply=%region_1.1 | all-reduce | flops 2048 | bytes 16384 | tf_op jit(solution)/shard_map/while/body/eval_jaxpr/psum | solution.py:40
  249.1 56.2 %collective-permute-start = (f32[64,32]{0,1:T(8,128)S(1)}, f32[64,32]{0,1:T(8,128)S(1)}, u32[]{:S(2)}, u32[]{:S(2)}) collective-permute-start(f32[64,32]{0,1:T(8,128)S(1)} %multiply_subtract_fusion.7), channel_id=1, source_target_pairs={{0,7},{1,0},{2,1},{3,2},{4,3},{5,4},{6,5},{7,6},{8,15},{9,8},{10,9... | collective-permute-start | bytes 24584 | tf_op jit(solution)/shard_map/while/body/eval_jaxpr/ppermute | solution.py:43
  310.7 56.1 %psum.60 = f32[64,32]{0,1:T(8,128)S(1)} all-reduce(f32[64,32]{0,1:T(8,128)S(1)} %fusion.110), channel_id=1, replica_groups=mesh['rep'=1,'sub'=16,'blk'=8] {'sub'}, use_global_device_ids=true, to_apply=%region_1.1 | all-reduce | flops 2048 | bytes 16384 | tf_op jit(solution)/shard_map/while/body/eval_jaxpr/psum | solution.py:40
  368.5 56.0 %psum.61 = f32[64,32]{0,1:T(8,128)S(1)} all-reduce(f32[64,32]{0,1:T(8,128)S(1)} %fusion.114), channel_id=1, replica_groups=mesh['rep'=1,'sub'=16,'blk'=8] {'sub'}, use_global_device_ids=true, to_apply=%region_2.2 | all-reduce | flops 2048 | bytes 16384 | tf_op jit(solution)/shard_map/while/body/eval_jaxpr/psum | solution.py:40
  426.2 55.9 %psum.62 = f32[64,32]{0,1:T(8,128)S(1)} all-reduce(f32[64,32]{0,1:T(8,128)S(1)} %fusion.117), channel_id=1, replica_groups=mesh['rep'=1,'sub'=16,'blk'=8] {'sub'}, use_global_device_ids=true, to_apply=%region_3.3 | all-reduce | flops 2048 | bytes 16384 | tf_op jit(solution)/shard_map/while/body/eval_jaxpr/psum | solution.py:40
  598.1 56.1 %psum.60 = f32[64,32]{0,1:T(8,128)S(1)} all-reduce(f32[64,32]{0,1:T(8,128)S(1)} %fusion.110), channel_id=1, replica_groups=mesh['rep'=1,'sub'=16,'blk'=8] {'sub'}, use_global_device_ids=true, to_apply=%region_1.1 | all-reduce | flops 2048 | bytes 16384 | tf_op jit(solution)/shard_map/while/body/eval_jaxpr/psum | solution.py:40
  656.0 56.0 %psum.61 = f32[64,32]{0,1:T(8,128)S(1)} all-reduce(f32[64,32]{0,1:T(8,128)S(1)} %fusion.114), channel_id=1, replica_groups=mesh['rep'=1,'sub'=16,'blk'=8] {'sub'}, use_global_device_ids=true, to_apply=%region_2.2 | all-reduce | flops 2048 | bytes 16384 | tf_op jit(solution)/shard_map/while/body/eval_jaxpr/psum | solution.py:40
  713.7 55.9 %psum.62 = f32[64,32]{0,1:T(8,128)S(1)} all-reduce(f32[64,32]{0,1:T(8,128)S(1)} %fusion.117), channel_id=1, replica_groups=mesh['rep'=1,'sub'=16,'blk'=8] {'sub'}, use_global_device_ids=true, to_apply=%region_3.3 | all-reduce | flops 2048 | bytes 16384 | tf_op jit(solution)/shard_map/while/body/eval_jaxpr/psum | solution.py:40
  885.6 56.1 %psum.60 = f32[64,32]{0,1:T(8,128)S(1)} all-reduce(f32[64,32]{0,1:T(8,128)S(1)} %fusion.110), channel_id=1, replica_groups=mesh['rep'=1,'sub'=16,'blk'=8] {'sub'}, use_global_device_ids=true, to_apply=%region_1.1 | all-reduce | flops 2048 | bytes 16384 | tf_op jit(solution)/shard_map/while/body/eval_jaxpr/psum | solution.py:40
  943.4 56.0 %psum.61 = f32[64,32]{0,1:T(8,128)S(1)} all-reduce(f32[64,32]{0,1:T(8,128)S(1)} %fusion.114), channel_id=1, replica_groups=mesh['rep'=1,'sub'=16,'blk'=8] {'sub'}, use_global_device_ids=true, to_apply=%region_2.2 | all-reduce | flops 2048 | bytes 16384 | tf_op jit(solution)/shard_map/while/body/eval_jaxpr/psum | solution.py:40
  1001.1 55.9 %psum.62 = f32[64,32]{0,1:T(8,128)S(1)} all-reduce(f32[64,32]{0,1:T(8,128)S(1)} %fusion.117), channel_id=1, replica_groups=mesh['rep'=1,'sub'=16,'blk'=8] {'sub'}, use_global_device_ids=true, to_apply=%region_3.3 | all-reduce | flops 2048 | bytes 16384 | tf_op jit(solution)/shard_map/while/body/eval_jaxpr/psum | solution.py:40
  1173.0 56.1 %psum.60 = f32[64,32]{0,1:T(8,128)S(1)} all-reduce(f32[64,32]{0,1:T(8,128)S(1)} %fusion.110), channel_id=1, replica_groups=mesh['rep'=1,'sub'=16,'blk'=8] {'sub'}, use_global_device_ids=true, to_apply=%region_1.1 | all-reduce | flops 2048 | bytes 16384 | tf_op jit(solution)/shard_map/while/body/eval_jaxpr/psum | solution.py:40
  1230.9 56.0 %psum.61 = f32[64,32]{0,1:T(8,128)S(1)} all-reduce(f32[64,32]{0,1:T(8,128)S(1)} %fusion.114), channel_id=1, replica_groups=mesh['rep'=1,'sub'=16,'blk'=8] {'sub'}, use_global_device_ids=true, to_apply=%region_2.2 | all-reduce | flops 2048 | bytes 16384 | tf_op jit(solution)/shard_map/while/body/eval_jaxpr/psum | solution.py:40
  1460.4 56.1 %psum.60 = f32[64,32]{0,1:T(8,128)S(1)} all-reduce(f32[64,32]{0,1:T(8,128)S(1)} %fusion.110), channel_id=1, replica_groups=mesh['rep'=1,'sub'=16,'blk'=8] {'sub'}, use_global_device_ids=true, to_apply=%region_1.1 | all-reduce | flops 2048 | bytes 16384 | tf_op jit(solution)/shard_map/while/body/eval_jaxpr/psum | solution.py:40
  1518.3 56.0 %psum.61 = f32[64,32]{0,1:T(8,128)S(1)} all-reduce(f32[64,32]{0,1:T(8,128)S(1)} %fusion.114), channel_id=1, replica_groups=mesh['rep'=1,'sub'=16,'blk'=8] {'sub'}, use_global_device_ids=true, to_apply=%region_2.2 | all-reduce | flops 2048 | bytes 16384 | tf_op jit(solution)/shard_map/while/body/eval_jaxpr/psum | solution.py:40
  1576.0 55.9 %psum.62 = f32[64,32]{0,1:T(8,128)S(1)} all-reduce(f32[64,32]{0,1:T(8,128)S(1)} %fusion.117), channel_id=1, replica_groups=mesh['rep'=1,'sub'=16,'blk'=8] {'sub'}, use_global_device_ids=true, to_apply=%region_3.3 | all-reduce | flops 2048 | bytes 16384 | tf_op jit(solution)/shard_map/while/body/eval_jaxpr/psum | solution.py:40
  1862.6 55.9 %psum.62 = f32[64,32]{0,1:T(8,128)S(1)} all-reduce(f32[64,32]{0,1:T(8,128)S(1)} %fusion.117), channel_id=1, replica_groups=mesh['rep'=1,'sub'=16,'blk'=8] {'sub'}, use_global_device_ids=true, to_apply=%region_3.3 | all-reduce | flops 2048 | bytes 16384 | tf_op jit(solution)/shard_map/while/body/eval_jaxpr/psum | solution.py:40
  2437.4 55.9 %psum.62 = f32[64,32]{0,1:T(8,128)S(1)} all-reduce(f32[64,32]{0,1:T(8,128)S(1)} %fusion.117), channel_id=1, replica_groups=mesh['rep'=1,'sub'=16,'blk'=8] {'sub'}, use_global_device_ids=true, to_apply=%region_3.3 | all-reduce | flops 2048 | bytes 16384 | tf_op jit(solution)/shard_map/while/body/eval_jaxpr/psum | solution.py:40
  2724.8 55.9 %psum.62 = f32[64,32]{0,1:T(8,128)S(1)} all-reduce(f32[64,32]{0,1:T(8,128)S(1)} %fusion.117), channel_id=1, replica_groups=mesh['rep'=1,'sub'=16,'blk'=8] {'sub'}, use_global_device_ids=true, to_apply=%region_3.3 | all-reduce | flops 2048 | bytes 16384 | tf_op jit(solution)/shard_map/while/body/eval_jaxpr/psum | solution.py:40
  3012.3 55.9 %psum.62 = f32[64,32]{0,1:T(8,128)S(1)} all-reduce(f32[64,32]{0,1:T(8,128)S(1)} %fusion.117), channel_id=1, replica_groups=mesh['rep'=1,'sub'=16,'blk'=8] {'sub'}, use_global_device_ids=true, to_apply=%region_3.3 | all-reduce | flops 2048 | bytes 16384 | tf_op jit(solution)/shard_map/while/body/eval_jaxpr/psum | solution.py:40
  3587.1 55.9 %psum.62 = f32[64,32]{0,1:T(8,128)S(1)} all-reduce(f32[64,32]{0,1:T(8,128)S(1)} %fusion.117), channel_id=1, replica_groups=mesh['rep'=1,'sub'=16,'blk'=8] {'sub'}, use_global_device_ids=true, to_apply=%region_3.3 | all-reduce | flops 2048 | bytes 16384 | tf_op jit(solution)/shard_map/while/body/eval_jaxpr/psum | solution.py:40
  3874.5 55.9 %psum.62 = f32[64,32]{0,1:T(8,128)S(1)} all-reduce(f32[64,32]{0,1:T(8,128)S(1)} %fusion.117), channel_id=1, replica_groups=mesh['rep'=1,'sub'=16,'blk'=8] {'sub'}, use_global_device_ids=true, to_apply=%region_3.3 | all-reduce | flops 2048 | bytes 16384 | tf_op jit(solution)/shard_map/while/body/eval_jaxpr/psum | solution.py:40
  4449.4 55.9 %psum.62 = f32[64,32]{0,1:T(8,128)S(1)} all-reduce(f32[64,32]{0,1:T(8,128)S(1)} %fusion.117), channel_id=1, replica_groups=mesh['rep'=1,'sub'=16,'blk'=8] {'sub'}, use_global_device_ids=true, to_apply=%region_3.3 | all-reduce | flops 2048 | bytes 16384 | tf_op jit(solution)/shard_map/while/body/eval_jaxpr/psum | solution.py:40
  (354 shorter events, 3323.4 us)
Async XLA Ops:
  6.0 5.4 copy-start.1
  6.0 5.4 copy-start.2
  249.1 58.7 %collective-permute-start = (f32[64,32]{0,1:T(8,128)S(1)}, f32[64,32]{0,1:T(8,128)S(1)}, u32[]{:S(2)}, u32[]{:S(2)}) collective-permute-start(f32[64,32]{0,1:T(8,128)S(1)} %multiply_subtract_fusion.7), channel_id=1, source_target_pairs={{0,7},{1,0},{2,1},{3,2},{4,3},{5,4},{6,5},{7,6},{8,15},{9,8},{10,9... | collective-permute-start | bytes 24584 | tf_op jit(solution)/shard_map/while/body/eval_jaxpr/ppermute | solution.py:43
  539.6 55.7 %collective-permute-start = (f32[64,32]{0,1:T(8,128)S(1)}, f32[64,32]{0,1:T(8,128)S(1)}, u32[]{:S(2)}, u32[]{:S(2)}) collective-permute-start(f32[64,32]{0,1:T(8,128)S(1)} %multiply_subtract_fusion.7), channel_id=1, source_target_pairs={{0,7},{1,0},{2,1},{3,2},{4,3},{5,4},{6,5},{7,6},{8,15},{9,8},{10,9... | collective-permute-start | bytes 24584 | tf_op jit(solution)/shard_map/while/body/eval_jaxpr/ppermute | solution.py:43
  827.0 55.7 %collective-permute-start = (f32[64,32]{0,1:T(8,128)S(1)}, f32[64,32]{0,1:T(8,128)S(1)}, u32[]{:S(2)}, u32[]{:S(2)}) collective-permute-start(f32[64,32]{0,1:T(8,128)S(1)} %multiply_subtract_fusion.7), channel_id=1, source_target_pairs={{0,7},{1,0},{2,1},{3,2},{4,3},{5,4},{6,5},{7,6},{8,15},{9,8},{10,9... | collective-permute-start | bytes 24584 | tf_op jit(solution)/shard_map/while/body/eval_jaxpr/ppermute | solution.py:43
  1114.5 55.7 %collective-permute-start = (f32[64,32]{0,1:T(8,128)S(1)}, f32[64,32]{0,1:T(8,128)S(1)}, u32[]{:S(2)}, u32[]{:S(2)}) collective-permute-start(f32[64,32]{0,1:T(8,128)S(1)} %multiply_subtract_fusion.7), channel_id=1, source_target_pairs={{0,7},{1,0},{2,1},{3,2},{4,3},{5,4},{6,5},{7,6},{8,15},{9,8},{10,9... | collective-permute-start | bytes 24584 | tf_op jit(solution)/shard_map/while/body/eval_jaxpr/ppermute | solution.py:43
  1401.9 55.7 %collective-permute-start = (f32[64,32]{0,1:T(8,128)S(1)}, f32[64,32]{0,1:T(8,128)S(1)}, u32[]{:S(2)}, u32[]{:S(2)}) collective-permute-start(f32[64,32]{0,1:T(8,128)S(1)} %multiply_subtract_fusion.7), channel_id=1, source_target_pairs={{0,7},{1,0},{2,1},{3,2},{4,3},{5,4},{6,5},{7,6},{8,15},{9,8},{10,9... | collective-permute-start | bytes 24584 | tf_op jit(solution)/shard_map/while/body/eval_jaxpr/ppermute | solution.py:43
  1689.4 55.6 %collective-permute-start = (f32[64,32]{0,1:T(8,128)S(1)}, f32[64,32]{0,1:T(8,128)S(1)}, u32[]{:S(2)}, u32[]{:S(2)}) collective-permute-start(f32[64,32]{0,1:T(8,128)S(1)} %multiply_subtract_fusion.7), channel_id=1, source_target_pairs={{0,7},{1,0},{2,1},{3,2},{4,3},{5,4},{6,5},{7,6},{8,15},{9,8},{10,9... | collective-permute-start | bytes 24584 | tf_op jit(solution)/shard_map/while/body/eval_jaxpr/ppermute | solution.py:43
  1975.9 56.5 %collective-permute-start = (f32[64,32]{0,1:T(8,128)S(1)}, f32[64,32]{0,1:T(8,128)S(1)}, u32[]{:S(2)}, u32[]{:S(2)}) collective-permute-start(f32[64,32]{0,1:T(8,128)S(1)} %multiply_subtract_fusion.7), channel_id=1, source_target_pairs={{0,7},{1,0},{2,1},{3,2},{4,3},{5,4},{6,5},{7,6},{8,15},{9,8},{10,9... | collective-permute-start | bytes 24584 | tf_op jit(solution)/shard_map/while/body/eval_jaxpr/ppermute | solution.py:43
  2263.4 56.5 %collective-permute-start = (f32[64,32]{0,1:T(8,128)S(1)}, f32[64,32]{0,1:T(8,128)S(1)}, u32[]{:S(2)}, u32[]{:S(2)}) collective-permute-start(f32[64,32]{0,1:T(8,128)S(1)} %multiply_subtract_fusion.7), channel_id=1, source_target_pairs={{0,7},{1,0},{2,1},{3,2},{4,3},{5,4},{6,5},{7,6},{8,15},{9,8},{10,9... | collective-permute-start | bytes 24584 | tf_op jit(solution)/shard_map/while/body/eval_jaxpr/ppermute | solution.py:43
  2550.8 56.5 %collective-permute-start = (f32[64,32]{0,1:T(8,128)S(1)}, f32[64,32]{0,1:T(8,128)S(1)}, u32[]{:S(2)}, u32[]{:S(2)}) collective-permute-start(f32[64,32]{0,1:T(8,128)S(1)} %multiply_subtract_fusion.7), channel_id=1, source_target_pairs={{0,7},{1,0},{2,1},{3,2},{4,3},{5,4},{6,5},{7,6},{8,15},{9,8},{10,9... | collective-permute-start | bytes 24584 | tf_op jit(solution)/shard_map/while/body/eval_jaxpr/ppermute | solution.py:43
  2838.2 56.5 %collective-permute-start = (f32[64,32]{0,1:T(8,128)S(1)}, f32[64,32]{0,1:T(8,128)S(1)}, u32[]{:S(2)}, u32[]{:S(2)}) collective-permute-start(f32[64,32]{0,1:T(8,128)S(1)} %multiply_subtract_fusion.7), channel_id=1, source_target_pairs={{0,7},{1,0},{2,1},{3,2},{4,3},{5,4},{6,5},{7,6},{8,15},{9,8},{10,9... | collective-permute-start | bytes 24584 | tf_op jit(solution)/shard_map/while/body/eval_jaxpr/ppermute | solution.py:43
  3125.6 56.5 %collective-permute-start = (f32[64,32]{0,1:T(8,128)S(1)}, f32[64,32]{0,1:T(8,128)S(1)}, u32[]{:S(2)}, u32[]{:S(2)}) collective-permute-start(f32[64,32]{0,1:T(8,128)S(1)} %multiply_subtract_fusion.7), channel_id=1, source_target_pairs={{0,7},{1,0},{2,1},{3,2},{4,3},{5,4},{6,5},{7,6},{8,15},{9,8},{10,9... | collective-permute-start | bytes 24584 | tf_op jit(solution)/shard_map/while/body/eval_jaxpr/ppermute | solution.py:43
  3413.0 56.5 %collective-permute-start = (f32[64,32]{0,1:T(8,128)S(1)}, f32[64,32]{0,1:T(8,128)S(1)}, u32[]{:S(2)}, u32[]{:S(2)}) collective-permute-start(f32[64,32]{0,1:T(8,128)S(1)} %multiply_subtract_fusion.7), channel_id=1, source_target_pairs={{0,7},{1,0},{2,1},{3,2},{4,3},{5,4},{6,5},{7,6},{8,15},{9,8},{10,9... | collective-permute-start | bytes 24584 | tf_op jit(solution)/shard_map/while/body/eval_jaxpr/ppermute | solution.py:43
  3700.4 56.5 %collective-permute-start = (f32[64,32]{0,1:T(8,128)S(1)}, f32[64,32]{0,1:T(8,128)S(1)}, u32[]{:S(2)}, u32[]{:S(2)}) collective-permute-start(f32[64,32]{0,1:T(8,128)S(1)} %multiply_subtract_fusion.7), channel_id=1, source_target_pairs={{0,7},{1,0},{2,1},{3,2},{4,3},{5,4},{6,5},{7,6},{8,15},{9,8},{10,9... | collective-permute-start | bytes 24584 | tf_op jit(solution)/shard_map/while/body/eval_jaxpr/ppermute | solution.py:43
  3987.9 56.5 %collective-permute-start = (f32[64,32]{0,1:T(8,128)S(1)}, f32[64,32]{0,1:T(8,128)S(1)}, u32[]{:S(2)}, u32[]{:S(2)}) collective-permute-start(f32[64,32]{0,1:T(8,128)S(1)} %multiply_subtract_fusion.7), channel_id=1, source_target_pairs={{0,7},{1,0},{2,1},{3,2},{4,3},{5,4},{6,5},{7,6},{8,15},{9,8},{10,9... | collective-permute-start | bytes 24584 | tf_op jit(solution)/shard_map/while/body/eval_jaxpr/ppermute | solution.py:43
  4275.3 56.5 %collective-permute-start = (f32[64,32]{0,1:T(8,128)S(1)}, f32[64,32]{0,1:T(8,128)S(1)}, u32[]{:S(2)}, u32[]{:S(2)}) collective-permute-start(f32[64,32]{0,1:T(8,128)S(1)} %multiply_subtract_fusion.7), channel_id=1, source_target_pairs={{0,7},{1,0},{2,1},{3,2},{4,3},{5,4},{6,5},{7,6},{8,15},{9,8},{10,9... | collective-permute-start | bytes 24584 | tf_op jit(solution)/shard_map/while/body/eval_jaxpr/ppermute | solution.py:43
  4562.7 56.5 %collective-permute-start = (f32[64,32]{0,1:T(8,128)S(1)}, f32[64,32]{0,1:T(8,128)S(1)}, u32[]{:S(2)}, u32[]{:S(2)}) collective-permute-start(f32[64,32]{0,1:T(8,128)S(1)} %multiply_subtract_fusion.7), channel_id=1, source_target_pairs={{0,7},{1,0},{2,1},{3,2},{4,3},{5,4},{6,5},{7,6},{8,15},{9,8},{10,9... | collective-permute-start | bytes 24584 | tf_op jit(solution)/shard_map/while/body/eval_jaxpr/ppermute | solution.py:43
  4619.2 0.7 copy-start
where the time goes:
time: 4630 us; the launch traced here: 4620 us
  blocking collectives  3580 us (77%)
  starting transfers between devices  863 us (19%)
  matrix products  108 us (2%)
    psum x64, blocking collectives, sub_epoch(): grad_item = lax.psum(part_item, 'sub') + decay_coef * item_st  3580 us
    ppermute x16, starting transfers between devices, sub_epoch(): return (user_st, lax.ppermute(item_st, 'blk', prev_pairs))  863 us
  transfers between devices with their start and end apart: 16, of which 16 were waited for; matrix products, arithmetic and copies ran while one was open for 0% of the time, Pallas kernels for 0%

commit v1 on v0

v1 whole, which is shorter than its diff:
```python
import functools
import math

import jax
import jax.numpy as jnp
from jax import lax
from jax.experimental import pallas as pl
from jax.experimental.pallas import tpu as pltpu
from jax.sharding import PartitionSpec as P

STEPS = 4
EPOCHS = 2
STEP_GAIN = 0.4
DECAY = 0.002
GROUPS = 4
MESH = pl.DeviceIdType.MESH
OFFSETS = ((2, 2), (2, 1), (2, 3), (1, 2), (3, 2), (1, 1), (1, 3), (3, 1), (3, 3), (2, 0), (0, 2), (1, 0), (3, 0), (0, 1), (0, 3))


def kernel(dims, r_hbm, m_hbm, ut_in, vt_in, ut_out, vt_out, rbuf, mbuf, packed, ut, uh, uth, wt, err, vst, xsend, slots, xslots, vslots,
           load_sem, send_sem, recv_sem, xsend_sem, xrecv_sem, vsend_sem, vrecv_sem):
    blk_n, sub_n, step_size, decay_coef = dims
    users = ut_in.shape[1]
    rows = users // GROUPS
    rank = ut_in.shape[0]
    half = rank // 2
    pairs = blk_n // 2
    me_b = lax.axis_index("blk")
    me_s = lax.axis_index("sub")
    me_z, me_y = me_s // 4, me_s % 4
    prev_b = (me_b + blk_n - 1) % blk_n
    next_b = (me_b + 1) % blk_n
    first_pair = me_b // 2

    def load(q, src, dst, sem):
        col = pl.multiple_of(((first_pair + q) % pairs) * 128, 128)
        return pltpu.make_async_copy(src.at[:, pl.ds(col, 128)], dst.at[q], load_sem.at[sem, q])

    for q in range(pairs):
        load(q, r_hbm, rbuf, 0).start()
        load(q, m_hbm, mbuf, 1).start()

    def at(dz, dy):
        return ((me_z + dz) % 4) * 4 + (me_y + dy) % 4

    barrier = pltpu.get_barrier_semaphore()
    for dz, dy in OFFSETS:
        pl.semaphore_signal(barrier, inc=1, device_id={"sub": at(dz, dy)}, device_id_type=MESH)
    for other in (prev_b, next_b):
        for dz, dy in OFFSETS + ((0, 0),):
            pl.semaphore_signal(barrier, inc=1, device_id={"sub": at(dz, dy), "blk": other}, device_id_type=MESH)

    low = lax.broadcasted_iota(jnp.int32, (half, 128), 1) < 64

    for g in range(GROUPS):
        piece = ut_in[:, g * rows:(g + 1) * rows]
        ut[g * rank:(g + 1) * rank, :] = piece
    first = ut[...].astype(jnp.bfloat16)
    uth[...] = first
    uh[...] = first.T
    vst[:, 0:64] = vt_in[0:half, :]
    vst[:, 64:128] = vt_in[half:rank, :]
    wt[...] = jnp.zeros_like(wt)

    chunk = 64
    low_c = lax.broadcasted_iota(jnp.int32, (chunk, 128), 1) < 64

    def pack_pair(q, carry):
        load(q, r_hbm, rbuf, 0).wait()
        load(q, m_hbm, mbuf, 1).wait()
        even = ((first_pair + q) % pairs) * 2

        def pack_rows(c, carry2):
            base = pl.multiple_of(c * chunk, chunk)
            for col in range(2):
                vals = []
                for g in (2 * col, 2 * col + 1):
                    src = pl.ds(g * rows + base, chunk)
                    vals.append(jnp.where(mbuf[q, src, :] != 0, rbuf[q, src, :], jnp.nan))
                x0, x1 = vals
                packed[even, pl.ds(base, chunk), col * 128:(col + 1) * 128] = jnp.where(low_c, x0, pltpu.roll(x1, 64, 1))
                packed[even + 1, pl.ds(base, chunk), col * 128:(col + 1) * 128] = jnp.where(low_c, pltpu.roll(x0, 64, 1), x1)
            return carry2

        lax.fori_loop(0, rows // chunk, pack_rows, 0)
        return carry

    lax.fori_loop(0, pairs, pack_pair, 0)
    pl.semaphore_wait(barrier, 3 * sub_n - 1)

    def spread(vp):
        swapped = pltpu.roll(vp, 64, 1)
        full = jnp.concatenate([jnp.where(low, vp, swapped), jnp.where(low, swapped, vp)], axis=0)
        left = lax.broadcasted_iota(jnp.int32, (rank, 128), 1) < 64
        lo = jnp.where(left, full, 0.0).astype(jnp.bfloat16)
        hi = jnp.where(left, 0.0, full).astype(jnp.bfloat16)
        wt[0:rank, 0:128] = lo
        wt[rank:2 * rank, 0:128] = hi
        wt[2 * rank:3 * rank, 128:256] = lo
        wt[3 * rank:4 * rank, 128:256] = hi

    def partial(block):
        for c in range(2):
            sl = slice(c * (rows // 2), (c + 1) * (rows // 2))
            predicted = jnp.dot(uh[sl, :], wt[...], preferred_element_type=jnp.float32)
            rate = packed[block, sl, :]
            err[sl, :] = jnp.where(rate == rate, predicted - rate, 0.0).astype(jnp.bfloat16)
        z = jnp.dot(uth[...], err[...], preferred_element_type=jnp.float32)
        s_lo = z[0:rank, 0:128] + z[2 * rank:3 * rank, 128:256]
        s_hi = z[rank:2 * rank, 0:128] + z[3 * rank:4 * rank, 128:256]
        left = lax.broadcasted_iota(jnp.int32, (rank, 128), 1) < 64
        both = jnp.where(left, s_lo, s_hi)
        top, bottom = both[0:half], both[half:rank]
        return jnp.where(low, top, bottom) + pltpu.roll(jnp.where(low, bottom, top), 64, 1)

    def user_step():
        grad = lax.dot_general(wt[...], err[...], (((1,), (1,)), ((), ())), preferred_element_type=jnp.float32)
        old = ut[...]
        new = old - step_size * (grad + decay_coef * old)
        ut[...] = new
        new_half = new.astype(jnp.bfloat16)
        uth[...] = new_half
        uh[...] = new_half.T

    def item_step(parts):
        total = parts[0]
        for s in range(1, sub_n):
            total = total + parts[s]
        old = vst[...]
        return old - step_size * (total + decay_coef * old)

    def sub_epoch(t, carry):
        block = (me_b + t) % blk_n
        for step in range(STEPS - 1):
            spread(vst[...])
            slots[step, me_s] = partial(block)
            copies = []
            for dz, dy in OFFSETS:
                copy = pltpu.make_async_remote_copy(
                    src_ref=slots.at[step, me_s], dst_ref=slots.at[step, me_s], send_sem=send_sem.at[step], recv_sem=recv_sem.at[step],
                    device_id={"sub": at(dz, dy)}, device_id_type=MESH)
                copy.start()
                copies.append(copy)
            user_step()
            everyone = slots.at[step, pl.ds(0, sub_n - 1)]
            pltpu.make_async_copy(everyone, everyone, send_sem.at[step]).wait()
            pltpu.make_async_copy(everyone, everyone, recv_sem.at[step]).wait()
            vst[...] = item_step(slots[step])
        ahead = pltpu.make_async_remote_copy(
            src_ref=vst, dst_ref=vslots.at[t], send_sem=vsend_sem, recv_sem=vrecv_sem.at[t],
            device_id={"blk": prev_b}, device_id_type=MESH)
        ahead.start()
        spread(vst[...])
        xsend[...] = partial(block)
        for dz, dy in OFFSETS + ((0, 0),):
            pltpu.make_async_remote_copy(
                src_ref=xsend, dst_ref=xslots.at[t, me_s], send_sem=xsend_sem, recv_sem=xrecv_sem.at[t],
                device_id={"sub": at(dz, dy), "blk": prev_b}, device_id_type=MESH).start()
        user_step()
        everyone = xslots.at[t]
        pltpu.make_async_copy(everyone, everyone, xsend_sem).wait()
        ahead.wait()
        pltpu.make_async_copy(everyone, everyone, xrecv_sem.at[t]).wait()
        vst[...] = vslots[t]
        vst[...] = item_step(xslots[t])
        return carry

    lax.fori_loop(0, EPOCHS * blk_n, sub_epoch, 0)

    for g in range(GROUPS):
        ut_out[:, g * rows:(g + 1) * rows] = ut[g * rank:(g + 1) * rank, :]
    vt_out[0:half, :] = vst[:, 0:64]
    vt_out[half:rank, :] = vst[:, 64:128]


def solution(mesh):
    blk_n = mesh.shape["blk"]
    sub_n = mesh.shape["sub"]
    row_spec = P(("rep", "blk", "sub"), None)
    item_spec = P(("rep", "blk"), None)

    def local_run(ratings, mask, user_init, item_init):
        users = ratings.shape[0]
        items, rank = item_init.shape
        big_side = max(items, sub_n * users)
        step_size = STEP_GAIN * math.sqrt(rank) / (math.sqrt(big_side) + math.sqrt(rank)) ** 2
        decay_coef = DECAY / step_size
        rows = users // GROUPS
        turns = EPOCHS * blk_n
        half = rank // 2
        vmem = pl.BlockSpec(memory_space=pltpu.VMEM)
        ut, vt = pl.pallas_call(
            functools.partial(kernel, (blk_n, sub_n, step_size, decay_coef)),
            out_shape=(jax.ShapeDtypeStruct((rank, users), jnp.float32), jax.ShapeDtypeStruct((rank, items), jnp.float32)),
            in_specs=[pl.BlockSpec(memory_space=pl.ANY)] * 2 + [vmem] * 2,
            out_specs=(vmem, vmem),
            scratch_shapes=[
                pltpu.VMEM((blk_n // 2, users, 128), jnp.float32),
                pltpu.VMEM((blk_n // 2, users, 128), jnp.int32),
                pltpu.VMEM((blk_n, rows, GROUPS * items), jnp.float32),
                pltpu.VMEM((GROUPS * rank, rows), jnp.float32),
                pltpu.VMEM((rows, GROUPS * rank), jnp.bfloat16),
                pltpu.VMEM((GROUPS * rank, rows), jnp.bfloat16),
                pltpu.VMEM((GROUPS * rank, GROUPS * items), jnp.bfloat16),
                pltpu.VMEM((rows, GROUPS * items), jnp.bfloat16),
                pltpu.VMEM((half, 128), jnp.float32),
                pltpu.VMEM((half, 128), jnp.float32),
                pltpu.VMEM((STEPS - 1, sub_n, half, 128), jnp.float32),
                pltpu.VMEM((turns, sub_n, half, 128), jnp.float32),
                pltpu.VMEM((turns, half, 128), jnp.float32),
                pltpu.SemaphoreType.DMA((2, blk_n // 2)),
                pltpu.SemaphoreType.DMA((STEPS - 1,)),
                pltpu.SemaphoreType.DMA((STEPS - 1,)),
                pltpu.SemaphoreType.DMA,
                pltpu.SemaphoreType.DMA((turns,)),
                pltpu.SemaphoreType.DMA,
                pltpu.SemaphoreType.DMA((turns,)),
            ],
            compiler_params=pltpu.CompilerParams(collective_id=0, has_side_effects=True, vmem_limit_bytes=48 * 1024 * 1024),
        )(ratings, mask, user_init.T, item_init.T)
        return ut.T, vt.T

    return jax.shard_map(local_run, mesh=mesh, in_specs=(row_spec, row_spec, row_spec, item_spec), out_specs=(row_spec, item_spec), check_vma=False)
```

time: 4630 us -> 342 us (0.07)
  blocking collectives: 3580 us -> 0 us
  starting transfers between devices: 863 us -> 0 us
  Pallas kernels: 0 us -> 336 us
  matrix products: 108 us -> 0 us
    psum x64 -> x0, blocking collectives: 3580 us -> none  [sub_epoch(): grad_item = lax.psum(part_item, 'sub') + decay_coef * item_st]
    ppermute x16 -> x0, starting transfers between devices: 863 us -> none  [sub_epoch(): return (user_st, lax.ppermute(item_st, 'blk', prev_pairs))]
    pallas_call x0 -> x1, Pallas kernels: none -> 336 us  [local_run(): pl.pallas_call(functools.partial(kernel, (blk_n, sub_n, step_size, decay_...]
    dot_general x192 -> x0, matrix products: 108 us -> none  [the longest x64 84.7 us: sub_epoch(): lax.dot_general(user_half, item_half, (((1,), (1,)), ((), ())), preferred...]
  transfers between devices with their start and end apart: 16 -> 0, of which waited for: 16 -> 0; matrix products, arithmetic and copies ran while one was open for 0% -> 0% of each run, Pallas kernels for 0% -> 0%
where the time goes in v1:
time: 342 us
  Pallas kernels  336 us (98%)
  local copies, waits for them, and re-layouts  5.16 us (2%)
    pallas_call x1, Pallas kernels, local_run(): pl.pallas_call(functools.partial(kernel, (blk_n, sub_n, step_size, decay_...  336 us

profile of v1, /device:TPU:1, one launch (start us, length us, event | category | flops | bytes accessed | tf_op | source)
XLA Modules:
  0.0 342.2 jit_solution(7015704914669469250)
XLA Ops:
  0.6 0.0 copy-start
  0.6 2.2 copy-done
  2.8 0.0 copy-start.1
  2.8 0.9 copy-done.1
  3.8 0.0 copy-start.2
  3.8 0.7 copy-done.2
  4.5 336.4 %shard_map.59 = (f32[32,2048]{1,0:T(8,128)S(1)}, f32[32,64]{1,0:T(8,128)S(1)}) custom-call(f32[2048,512]{1,0:T(8,128)S(1)} %copy-done, s32[2048,512]{1,0:T(8,128)} %m_hbm.1, f32[32,2048]{1,0:T(8,128)S(1)} %bitcast.4, f32[32,64]{1,0:T(8,128)S(1)} %bitcast.6), custom_call_target="tpu_custom_call" | custom-call | tf_op jit(solution)/shard_map/pallas_call | solution.py:192
  340.9 0.7 copy.8
  341.6 0.6 copy.9
Async XLA Ops:
  0.6 2.2 copy-start
  2.8 0.9 copy-start.1
  3.8 0.7 copy-start.2

commit v2 on v1

v2 whole, which is shorter than its diff:
```python
import functools
import math

import jax
import jax.numpy as jnp
from jax import lax
from jax.experimental import pallas as pl
from jax.experimental.pallas import tpu as pltpu
from jax.sharding import PartitionSpec as P

STEPS = 4
EPOCHS = 2
STEP_GAIN = 0.4
DECAY = 0.002
GROUPS = 4
TEAM = 4
PIECES = 4
MESH = pl.DeviceIdType.MESH


def kernel(dims, r_hbm, m_hbm, u_hbm, v_hbm, ut_out, vt_out, rbuf, mbuf, ubuf, vbuf, packed, work, usrc, uret, vown, vret, ut, uh, uth, wt, err, vst,
           xsend, slots, xslots, vslots, load_sem, ship_send, ship_recv, user_send, user_recv, item_send, item_recv, back_send, back_recv,
           final_send, final_recv, send_sem, recv_sem, xsend_sem, xrecv_sem, vsend_sem, vrecv_sem):
    blk_n, step_size, decay_coef = dims
    rank, users = ubuf.shape
    rows = users // GROUPS
    half = rank // 2
    pairs = blk_n // 2
    me_b = lax.axis_index("blk")
    me_s = lax.axis_index("sub")
    x, core = me_b // 2, me_b % 2
    z, y = me_s // 4, me_s % 4

    out_y = (y // 2 + core + x) % 2
    out_z = z // 2
    piece = 2 * out_y + out_z
    target = {"sub": (z + out_z * (3 - 2 * z)) * 4 + y + out_y * (3 - 2 * y), "blk": 2 * x + 1}
    is_own = jnp.logical_and(core == 1, piece == 0)
    ships = jnp.logical_not(is_own)
    is_worker = jnp.logical_and(core == 1, z < 2)
    job_core = (y // 2 + x) % 2
    job = 2 * x + job_core
    has_own = job_core == 1
    place = (z % 2) * 2 + y % 2

    def source(q):
        oy, oz = q // 2, q % 2
        return {"sub": (z + oz * (3 - 2 * z)) * 4 + y + oy * (3 - 2 * y), "blk": job}

    def worker(block, p):
        bx = block // 2
        return {"sub": (p // 2) * 4 + 2 * ((block % 2 + bx) % 2) + p % 2, "blk": 2 * bx + 1}

    prev_job = (job + blk_n - 1) % blk_n
    next_job = (job + 1) % blk_n

    def mate(d):
        dz, dy = d // 2, d % 2
        pz, py = (place // 2 + dz) % 2, (place % 2 + dy) % 2
        return pz * 2 + py

    def load(q, src, dst, kind):
        col = pl.multiple_of(((x + q) % pairs) * 128, 128)
        return pltpu.make_async_copy(src.at[:, pl.ds(col, 128)], dst.at[q], load_sem.at[kind, q])

    load_users = pltpu.make_async_copy(u_hbm, ubuf, load_sem.at[2, 0])
    load_items = pltpu.make_async_copy(v_hbm, vbuf, load_sem.at[2, 1])
    load_users.start()
    load_items.start()
    for q in range(pairs):
        load(q, r_hbm, rbuf, 0).start()
        load(q, m_hbm, mbuf, 1).start()

    barrier = pltpu.get_barrier_semaphore()

    def greet(device):
        pl.semaphore_signal(barrier, inc=1, device_id=device, device_id_type=MESH)

    @pl.when(ships)
    def _():
        greet(target)

    @pl.when(is_worker)
    def _():
        for q in range(1, PIECES):
            greet(source(q))

        @pl.when(jnp.logical_not(has_own))
        def _():
            greet(source(0))

        for d in (3, 2, 1):
            greet(worker(job, mate(d)))
        for p in range(TEAM):
            greet(worker(prev_job, p))
            greet(worker(next_job, p))

    low = lax.broadcasted_iota(jnp.int32, (half, 128), 1) < 64
    left = lax.broadcasted_iota(jnp.int32, (rank, 128), 1) < 64

    load_users.wait()
    for g in range(GROUPS):
        usrc[g * rank:(g + 1) * rank, :] = ubuf[:, g * rows:(g + 1) * rows]
    load_items.wait()
    vown[:, 0:64] = vbuf[0:half, :]
    vown[:, 64:128] = vbuf[half:rank, :]

    @pl.when(jnp.logical_not(is_worker))
    def _():
        pl.semaphore_wait(barrier, 1)

    @pl.when(jnp.logical_and(is_worker, has_own))
    def _():
        pl.semaphore_wait(barrier, PIECES - 1 + TEAM - 1 + 2 * TEAM)

    @pl.when(jnp.logical_and(is_worker, jnp.logical_not(has_own)))
    def _():
        pl.semaphore_wait(barrier, PIECES + 1 + TEAM - 1 + 2 * TEAM)

    send_users = pltpu.make_async_remote_copy(
        src_ref=usrc, dst_ref=ut.at[piece], send_sem=user_send, recv_sem=user_recv, device_id=target, device_id_type=MESH)
    send_items = pltpu.make_async_remote_copy(
        src_ref=vown, dst_ref=vst, send_sem=item_send, recv_sem=item_recv, device_id=target, device_id_type=MESH)
    gives_items = jnp.logical_and(core == 0, piece == 0)

    @pl.when(ships)
    def _():
        send_users.start()

    @pl.when(gives_items)
    def _():
        send_items.start()

    def ship(k):
        column = (me_b + k) % blk_n
        return pltpu.make_async_remote_copy(
            src_ref=packed.at[column], dst_ref=work.at[column, piece], send_sem=ship_send.at[k], recv_sem=ship_recv.at[column],
            device_id=target, device_id_type=MESH)

    chunk = 64
    low_c = lax.broadcasted_iota(jnp.int32, (chunk, 128), 1) < 64

    def pack_pair(q):
        load(q, r_hbm, rbuf, 0).wait()
        load(q, m_hbm, mbuf, 1).wait()
        even = ((x + q) % pairs) * 2

        def pack_rows(c, carry):
            base = pl.multiple_of(c * chunk, chunk)
            for col in range(2):
                vals = []
                for g in (2 * col, 2 * col + 1):
                    src = pl.ds(g * rows + base, chunk)
                    vals.append(jnp.where(mbuf[q, src, :] != 0, rbuf[q, src, :], jnp.nan))
                x0, x1 = vals
                packed[even, pl.ds(base, chunk), col * 128:(col + 1) * 128] = jnp.where(low_c, x0, pltpu.roll(x1, 64, 1))
                packed[even + 1, pl.ds(base, chunk), col * 128:(col + 1) * 128] = jnp.where(low_c, pltpu.roll(x0, 64, 1), x1)
            return carry

        lax.fori_loop(0, rows // chunk, pack_rows, 0)

    pack_pair(0)

    @pl.when(ships)
    def _():
        ship(0).start()

    def pack_rest(q, carry):
        pack_pair(q)
        return carry

    lax.fori_loop(1, pairs, pack_rest, 0)

    @pl.when(ships)
    def _():
        ship(1).start()

    @pl.when(jnp.logical_and(ships, jnp.logical_not(is_worker)))
    def _():
        def ship_next(k, carry):
            ship(k - 2).wait_send()
            ship(k).start()
            return carry

        lax.fori_loop(2, blk_n, ship_next, 0)
        ship(blk_n - 2).wait_send()
        ship(blk_n - 1).wait_send()

    @pl.when(is_own)
    def _():
        def keep(column, carry):
            work[column, 0] = packed[column]
            return carry

        lax.fori_loop(0, blk_n, keep, 0)
        ut[0] = usrc[...]
        vst[...] = vown[...]

    def halves(q):
        new_half = ut[q].astype(jnp.bfloat16)
        uth[:, q * rows:(q + 1) * rows] = new_half
        uh[q * rows:(q + 1) * rows, :] = new_half.T

    def spread(vp):
        swapped = pltpu.roll(vp, 64, 1)
        full = jnp.concatenate([jnp.where(low, vp, swapped), jnp.where(low, swapped, vp)], axis=0)
        lo = jnp.where(left, full, 0.0).astype(jnp.bfloat16)
        hi = jnp.where(left, 0.0, full).astype(jnp.bfloat16)
        wt[0:rank, 0:128] = lo
        wt[rank:2 * rank, 0:128] = hi
        wt[2 * rank:3 * rank, 128:256] = lo
        wt[3 * rank:4 * rank, 128:256] = hi

    def partial(block):
        for q in range(PIECES):
            sl = slice(q * rows, (q + 1) * rows)
            predicted = jnp.dot(uh[sl, :], wt[...], preferred_element_type=jnp.float32)
            rate = work[block, q]
            err[sl, :] = jnp.where(rate == rate, predicted - rate, 0.0).astype(jnp.bfloat16)
        s = jnp.dot(uth[...], err[...], preferred_element_type=jnp.float32)
        s_lo = s[0:rank, 0:128] + s[2 * rank:3 * rank, 128:256]
        s_hi = s[rank:2 * rank, 0:128] + s[3 * rank:4 * rank, 128:256]
        both = jnp.where(left, s_lo, s_hi)
        top, bottom = both[0:half], both[half:rank]
        return jnp.where(low, top, bottom) + pltpu.roll(jnp.where(low, bottom, top), 64, 1)

    def user_step():
        for q in range(PIECES):
            grad = lax.dot_general(wt[...], err[q * rows:(q + 1) * rows, :], (((1,), (1,)), ((), ())), preferred_element_type=jnp.float32)
            old = ut[q]
            ut[q] = old - step_size * (grad + decay_coef * old)
            halves(q)

    def item_step(parts):
        total = (parts[0] + parts[1]) + (parts[2] + parts[3])
        old = vst[...]
        return old - step_size * (total + decay_coef * old)

    def await_pieces(buf, sem):
        @pl.when(has_own)
        def _():
            most = buf.at[pl.ds(1, PIECES - 1)]
            pltpu.make_async_copy(most, most, sem).wait()

        @pl.when(jnp.logical_not(has_own))
        def _():
            pltpu.make_async_copy(buf, buf, sem).wait()

    def sub_epoch(t, carry):
        block = (job + t) % blk_n

        @pl.when(t < blk_n)
        def _():
            await_pieces(work.at[block], ship_recv.at[block])

        @pl.when(jnp.logical_and(ships, t < blk_n - 2))
        def _():
            ship(t).wait_send()
            ship(t + 2).start()

        for step in range(STEPS - 1):
            spread(vst[...])
            slots[step, place] = partial(block)
            for d in (3, 2, 1):
                pltpu.make_async_remote_copy(
                    src_ref=slots.at[step, place], dst_ref=slots.at[step, place], send_sem=send_sem.at[step], recv_sem=recv_sem.at[step],
                    device_id=worker(job, mate(d)), device_id_type=MESH).start()
            user_step()
            others = slots.at[step, pl.ds(0, TEAM - 1)]
            pltpu.make_async_copy(others, others, send_sem.at[step]).wait()
            pltpu.make_async_copy(others, others, recv_sem.at[step]).wait()
            vst[...] = item_step(slots[step])
        ahead = pltpu.make_async_remote_copy(
            src_ref=vst, dst_ref=vslots.at[t], send_sem=vsend_sem, recv_sem=vrecv_sem.at[t],
            device_id=worker(prev_job, place), device_id_type=MESH)
        ahead.start()
        spread(vst[...])
        xsend[...] = partial(block)
        for d in (3, 2, 1, 0):
            pltpu.make_async_remote_copy(
                src_ref=xsend, dst_ref=xslots.at[t, place], send_sem=xsend_sem, recv_sem=xrecv_sem.at[t],
                device_id=worker(prev_job, mate(d)), device_id_type=MESH).start()
        user_step()
        everyone = xslots.at[t]
        pltpu.make_async_copy(everyone, everyone, xsend_sem).wait()
        ahead.wait()
        pltpu.make_async_copy(everyone, everyone, xrecv_sem.at[t]).wait()
        vst[...] = vslots[t]
        vst[...] = item_step(xslots[t])
        return carry

    def give_users(q):
        return pltpu.make_async_remote_copy(
            src_ref=ut.at[q], dst_ref=uret, send_sem=back_send.at[q], recv_sem=back_recv, device_id=source(q), device_id_type=MESH)

    def give_items(q):
        return pltpu.make_async_remote_copy(
            src_ref=vst, dst_ref=vret, send_sem=final_send.at[q], recv_sem=final_recv, device_id=source(q), device_id_type=MESH)

    @pl.when(is_worker)
    def _():
        wt[...] = jnp.zeros_like(wt)
        await_pieces(ut, user_recv)

        @pl.when(jnp.logical_not(has_own))
        def _():
            pltpu.make_async_copy(vst, vst, item_recv).wait()

        for q in range(PIECES):
            halves(q)
        lax.fori_loop(0, EPOCHS * blk_n, sub_epoch, 0)
        for q in (3, 2, 1):
            give_users(q).start()
            give_items(q).start()

        @pl.when(jnp.logical_not(has_own))
        def _():
            give_users(0).start()
            give_items(0).start()

        @pl.when(ships)
        def _():
            ship(blk_n - 2).wait_send()
            ship(blk_n - 1).wait_send()

    @pl.when(ships)
    def _():
        send_users.wait_send()
        pltpu.make_async_copy(uret, uret, back_recv).wait()
        pltpu.make_async_copy(vret, vret, final_recv).wait()
        for g in range(GROUPS):
            ut_out[:, g * rows:(g + 1) * rows] = uret[g * rank:(g + 1) * rank, :]
        vt_out[0:half, :] = vret[:, 0:64]
        vt_out[half:rank, :] = vret[:, 64:128]

    @pl.when(gives_items)
    def _():
        send_items.wait_send()

    @pl.when(is_own)
    def _():
        for g in range(GROUPS):
            ut_out[:, g * rows:(g + 1) * rows] = ut[0, g * rank:(g + 1) * rank, :]
        vt_out[0:half, :] = vst[:, 0:64]
        vt_out[half:rank, :] = vst[:, 64:128]

    @pl.when(is_worker)
    def _():
        for q in (3, 2, 1):
            give_users(q).wait_send()
            give_items(q).wait_send()

        @pl.when(jnp.logical_not(has_own))
        def _():
            give_users(0).wait_send()
            give_items(0).wait_send()


def solution(mesh):
    blk_n = mesh.shape["blk"]
    sub_n = mesh.shape["sub"]
    row_spec = P(("rep", "blk", "sub"), None)
    item_spec = P(("rep", "blk"), None)

    def local_run(ratings, mask, user_init, item_init):
        users = ratings.shape[0]
        items, rank = item_init.shape
        big_side = max(items, sub_n * users)
        step_size = STEP_GAIN * math.sqrt(rank) / (math.sqrt(big_side) + math.sqrt(rank)) ** 2
        decay_coef = DECAY / step_size
        rows = users // GROUPS
        turns = EPOCHS * blk_n
        half = rank // 2
        wide_u, wide_i = GROUPS * rank, GROUPS * items
        vmem = pl.BlockSpec(memory_space=pltpu.VMEM)
        dma = pltpu.SemaphoreType.DMA
        ut, vt = pl.pallas_call(
            functools.partial(kernel, (blk_n, step_size, decay_coef)),
            out_shape=(jax.ShapeDtypeStruct((rank, users), jnp.float32), jax.ShapeDtypeStruct((rank, items), jnp.float32)),
            in_specs=[pl.BlockSpec(memory_space=pl.ANY)] * 4,
            out_specs=(vmem, vmem),
            scratch_shapes=[
                pltpu.VMEM((blk_n // 2, users, 128), jnp.float32),
                pltpu.VMEM((blk_n // 2, users, 128), jnp.int32),
                pltpu.VMEM((rank, users), jnp.float32),
                pltpu.VMEM((rank, items), jnp.float32),
                pltpu.VMEM((blk_n, rows, wide_i), jnp.float32),
                pltpu.VMEM((blk_n, PIECES, rows, wide_i), jnp.float32),
                pltpu.VMEM((wide_u, rows), jnp.float32),
                pltpu.VMEM((wide_u, rows), jnp.float32),
                pltpu.VMEM((half, 128), jnp.float32),
                pltpu.VMEM((half, 128), jnp.float32),
                pltpu.VMEM((PIECES, wide_u, rows), jnp.float32),
                pltpu.VMEM((PIECES * rows, wide_u), jnp.bfloat16),
                pltpu.VMEM((wide_u, PIECES * rows), jnp.bfloat16),
                pltpu.VMEM((wide_u, wide_i), jnp.bfloat16),
                pltpu.VMEM((PIECES * rows, wide_i), jnp.bfloat16),
                pltpu.VMEM((half, 128), jnp.float32),
                pltpu.VMEM((half, 128), jnp.float32),
                pltpu.VMEM((STEPS - 1, TEAM, half, 128), jnp.float32),
                pltpu.VMEM((turns, TEAM, half, 128), jnp.float32),
                pltpu.VMEM((turns, half, 128), jnp.float32),
                dma((3, blk_n // 2)),
                dma((blk_n,)), dma((blk_n,)),
                dma, dma, dma, dma,
                dma((PIECES,)), dma,
                dma((PIECES,)), dma,
                dma((STEPS - 1,)), dma((STEPS - 1,)),
                dma, dma((turns,)),
                dma, dma((turns,)),
            ],
            compiler_params=pltpu.CompilerParams(collective_id=0, has_side_effects=True, vmem_limit_bytes=67043328),
        )(ratings, mask, user_init.T, item_init.T)
        return ut.T, vt.T

    return jax.shard_map(local_run, mesh=mesh, in_specs=(row_spec, row_spec, row_spec, item_spec), out_specs=(row_spec, item_spec), check_vma=False)
```

time: 342 us -> 289 us (0.85)
  Pallas kernels: 336 us -> 285 us
    pallas_call x1, Pallas kernels: 336 us -> 285 us  [local_run(): pl.pallas_call(functools.partial(kernel, (blk_n, step_size, decay_coef)),...]
where the time goes in v2:
time: 289 us
  Pallas kernels  285 us (99%)
  local copies, waits for them, and re-layouts  2.99 us (1%)
    pallas_call x1, Pallas kernels, local_run(): pl.pallas_call(functools.partial(kernel, (blk_n, step_size, decay_coef)),...  285 us

profile of v2, /device:TPU:1, one launch (start us, length us, event | category | flops | bytes accessed | tf_op | source)
XLA Modules:
  0.0 288.6 jit_solution(10078854015322046105)
XLA Ops:
  0.6 284.9 %shard_map.59 = (f32[32,2048]{1,0:T(8,128)}, f32[32,64]{1,0:T(8,128)}) custom-call(f32[2048,512]{1,0:T(8,128)} %r_hbm.1, s32[2048,512]{1,0:T(8,128)} %m_hbm.1, f32[32,2048]{1,0:T(8,128)} %bitcast.4, f32[32,64]{1,0:T(8,128)} %bitcast.6), custom_call_target="tpu_custom_call" | custom-call | tf_op jit(solution)/shard_map/pallas_call | solution.py:377
  285.6 1.7 copy.8
  287.2 1.3 copy.9

commit v3 on v2

--- a/solution.py
+++ b/solution.py
@@ -20,7 +20,7 @@
 
 def kernel(dims, r_hbm, m_hbm, u_hbm, v_hbm, ut_out, vt_out, rbuf, mbuf, ubuf, vbuf, packed, work, usrc, uret, vown, vret, ut, uh, uth, wt, err, vst,
            xsend, slots, xslots, vslots, load_sem, ship_send, ship_recv, user_send, user_recv, item_send, item_recv, back_send, back_recv,
-           final_send, final_recv, send_sem, recv_sem, xsend_sem, xrecv_sem, vsend_sem, vrecv_sem):
+           final_send, final_recv, send_sem, recv_sem, xsend_sem, xrecv_sem, vsend_sem, vrecv_sem, credit):
     blk_n, step_size, decay_coef = dims
     rank, users = ubuf.shape
     rows = users // GROUPS
@@ -171,11 +171,24 @@
 
     lax.fori_loop(1, pairs, pack_rest, 0)
 
-    @pl.when(ships)
+    is_far = piece == 3
+
+    @pl.when(is_far)
+    def _():
+        def ship_far(k, carry):
+            pl.semaphore_wait(credit, 1)
+            ship(k).start()
+            ship(k - 1).wait_send()
+            return carry
+
+        lax.fori_loop(1, blk_n, ship_far, 0)
+        ship(blk_n - 1).wait_send()
+
+    @pl.when(jnp.logical_and(ships, jnp.logical_not(is_far)))
     def _():
         ship(1).start()
 
-    @pl.when(jnp.logical_and(ships, jnp.logical_not(is_worker)))
+    @pl.when(jnp.logical_and(ships, jnp.logical_not(jnp.logical_or(is_worker, is_far))))
     def _():
         def ship_next(k, carry):
             ship(k - 2).wait_send()
@@ -252,6 +265,10 @@
         @pl.when(t < blk_n)
         def _():
             await_pieces(work.at[block], ship_recv.at[block])
+
+        @pl.when(t < blk_n - 1)
+        def _():
+            pl.semaphore_signal(credit, inc=1, device_id=source(3), device_id_type=MESH)
 
         @pl.when(jnp.logical_and(ships, t < blk_n - 2))
         def _():
@@ -408,6 +425,7 @@
                 dma((STEPS - 1,)), dma((STEPS - 1,)),
                 dma, dma((turns,)),
                 dma, dma((turns,)),
+                pltpu.SemaphoreType.REGULAR,
             ],
             compiler_params=pltpu.CompilerParams(collective_id=0, has_side_effects=True, vmem_limit_bytes=67043328),
         )(ratings, mask, user_init.T, item_init.T)

time: 289 us -> 249 us (0.86)
  Pallas kernels: 285 us -> 246 us
    pallas_call x1, Pallas kernels: 285 us -> 246 us  [local_run(): pl.pallas_call(functools.partial(kernel, (blk_n, step_size, decay_coef)),...]
where the time goes in v3:
time: 249 us
  Pallas kernels  246 us (99%)
  local copies, waits for them, and re-layouts  2.99 us (1%)
    pallas_call x1, Pallas kernels, local_run(): pl.pallas_call(functools.partial(kernel, (blk_n, step_size, decay_coef)),...  246 us

profile of v3, /device:TPU:1, one launch (start us, length us, event | category | flops | bytes accessed | tf_op | source)
XLA Modules:
  0.0 249.2 jit_solution(13005196928061384590)
XLA Ops:
  0.6 245.6 %shard_map.59 = (f32[32,2048]{1,0:T(8,128)}, f32[32,64]{1,0:T(8,128)}) custom-call(f32[2048,512]{1,0:T(8,128)} %r_hbm.1, s32[2048,512]{1,0:T(8,128)} %m_hbm.1, f32[32,2048]{1,0:T(8,128)} %bitcast.4, f32[32,64]{1,0:T(8,128)} %bitcast.6), custom_call_target="tpu_custom_call" | custom-call | tf_op jit(solution)/shard_map/pallas_call | solution.py:394
  246.2 1.7 copy.8
  247.9 1.3 copy.9

commit v4 on v3

--- a/solution.py
+++ b/solution.py
@@ -54,9 +54,9 @@
     prev_job = (job + blk_n - 1) % blk_n
     next_job = (job + 1) % blk_n
 
-    def mate(d):
+    def mate(d, flip=0):
         dz, dy = d // 2, d % 2
-        pz, py = (place // 2 + dz) % 2, (place % 2 + dy) % 2
+        pz, py = (place // 2 + dz) % 2, (place % 2 + dy + flip) % 2
         return pz * 2 + py
 
     def load(q, src, dst, kind):
@@ -67,9 +67,8 @@
     load_items = pltpu.make_async_copy(v_hbm, vbuf, load_sem.at[2, 1])
     load_users.start()
     load_items.start()
-    for q in range(pairs):
-        load(q, r_hbm, rbuf, 0).start()
-        load(q, m_hbm, mbuf, 1).start()
+    load(0, r_hbm, rbuf, 0).start()
+    load(0, m_hbm, mbuf, 1).start()
 
     barrier = pltpu.get_barrier_semaphore()
 
@@ -98,6 +97,11 @@
     low = lax.broadcasted_iota(jnp.int32, (half, 128), 1) < 64
     left = lax.broadcasted_iota(jnp.int32, (rank, 128), 1) < 64
 
+    load(0, r_hbm, rbuf, 0).wait()
+    load(0, m_hbm, mbuf, 1).wait()
+    for q in range(1, pairs):
+        load(q, r_hbm, rbuf, 0).start()
+        load(q, m_hbm, mbuf, 1).start()
     load_users.wait()
     for g in range(GROUPS):
         usrc[g * rank:(g + 1) * rank, :] = ubuf[:, g * rows:(g + 1) * rows]
@@ -141,8 +145,6 @@
     low_c = lax.broadcasted_iota(jnp.int32, (chunk, 128), 1) < 64
 
     def pack_pair(q):
-        load(q, r_hbm, rbuf, 0).wait()
-        load(q, m_hbm, mbuf, 1).wait()
         even = ((x + q) % pairs) * 2
 
         def pack_rows(c, carry):
@@ -166,6 +168,8 @@
         ship(0).start()
 
     def pack_rest(q, carry):
+        load(q, r_hbm, rbuf, 0).wait()
+        load(q, m_hbm, mbuf, 1).wait()
         pack_pair(q)
         return carry
 
@@ -258,6 +262,14 @@
         @pl.when(jnp.logical_not(has_own))
         def _():
             pltpu.make_async_copy(buf, buf, sem).wait()
+
+    def give_users(q):
+        return pltpu.make_async_remote_copy(
+            src_ref=ut.at[q], dst_ref=uret, send_sem=back_send.at[q], recv_sem=back_recv, device_id=source(q), device_id_type=MESH)
+
+    def give_items(q):
+        return pltpu.make_async_remote_copy(
+            src_ref=vst, dst_ref=vret, send_sem=final_send.at[q], recv_sem=final_recv, device_id=source(q), device_id_type=MESH)
 
     def sub_epoch(t, carry):
         block = (job + t) % blk_n
@@ -296,8 +308,18 @@
         for d in (3, 2, 1, 0):
             pltpu.make_async_remote_copy(
                 src_ref=xsend, dst_ref=xslots.at[t, place], send_sem=xsend_sem, recv_sem=xrecv_sem.at[t],
-                device_id=worker(prev_job, mate(d)), device_id_type=MESH).start()
+                device_id=worker(prev_job, mate(d, job_core)), device_id_type=MESH).start()
         user_step()
+
+        @pl.when(t == EPOCHS * blk_n - 1)
+        def _():
+            for q in (3, 1, 2):
+                give_users(q).start()
+
+            @pl.when(jnp.logical_not(has_own))
+            def _():
+                give_users(0).start()
+
         everyone = xslots.at[t]
         pltpu.make_async_copy(everyone, everyone, xsend_sem).wait()
         ahead.wait()
@@ -306,14 +328,6 @@
         vst[...] = item_step(xslots[t])
         return carry
 
-    def give_users(q):
-        return pltpu.make_async_remote_copy(
-            src_ref=ut.at[q], dst_ref=uret, send_sem=back_send.at[q], recv_sem=back_recv, device_id=source(q), device_id_type=MESH)
-
-    def give_items(q):
-        return pltpu.make_async_remote_copy(
-            src_ref=vst, dst_ref=vret, send_sem=final_send.at[q], recv_sem=final_recv, device_id=source(q), device_id_type=MESH)
-
     @pl.when(is_worker)
     def _():
         wt[...] = jnp.zeros_like(wt)
@@ -327,12 +341,10 @@
             halves(q)
         lax.fori_loop(0, EPOCHS * blk_n, sub_epoch, 0)
         for q in (3, 2, 1):
-            give_users(q).start()
             give_items(q).start()
 
         @pl.when(jnp.logical_not(has_own))
         def _():
-            give_users(0).start()
             give_items(0).start()
 
         @pl.when(ships)

time: 249 us -> 248 us (level)
  no operation moved by 1% of the time
where the time goes in v4:
time: 248 us; the launch traced here: 247 us
  Pallas kernels  244 us (98%)
  local copies, waits for them, and re-layouts  2.99 us (1%)
    pallas_call x1, Pallas kernels, local_run(): pl.pallas_call(functools.partial(kernel, (blk_n, step_size, decay_coef)),...  244 us

profile of v4, /device:TPU:1, one launch (start us, length us, event | category | flops | bytes accessed | tf_op | source)
XLA Modules:
  0.0 247.3 jit_solution(16532343056457663346)
XLA Ops:
  0.6 243.7 %shard_map.59 = (f32[32,2048]{1,0:T(8,128)}, f32[32,64]{1,0:T(8,128)}) custom-call(f32[2048,512]{1,0:T(8,128)} %r_hbm.1, s32[2048,512]{1,0:T(8,128)} %m_hbm.1, f32[32,2048]{1,0:T(8,128)} %bitcast.4, f32[32,64]{1,0:T(8,128)} %bitcast.6), custom_call_target="tpu_custom_call" | custom-call | tf_op jit(solution)/shard_map/pallas_call | solution.py:406
  244.3 1.7 copy.8
  246.0 1.3 copy.9

commit v5 on v4

--- a/solution.py
+++ b/solution.py
@@ -97,11 +97,6 @@
     low = lax.broadcasted_iota(jnp.int32, (half, 128), 1) < 64
     left = lax.broadcasted_iota(jnp.int32, (rank, 128), 1) < 64
 
-    load(0, r_hbm, rbuf, 0).wait()
-    load(0, m_hbm, mbuf, 1).wait()
-    for q in range(1, pairs):
-        load(q, r_hbm, rbuf, 0).start()
-        load(q, m_hbm, mbuf, 1).start()
     load_users.wait()
     for g in range(GROUPS):
         usrc[g * rank:(g + 1) * rank, :] = ubuf[:, g * rows:(g + 1) * rows]
@@ -161,6 +156,11 @@
 
         lax.fori_loop(0, rows // chunk, pack_rows, 0)
 
+    load(0, r_hbm, rbuf, 0).wait()
+    load(0, m_hbm, mbuf, 1).wait()
+    for q in range(1, pairs):
+        load(q, r_hbm, rbuf, 0).start()
+        load(q, m_hbm, mbuf, 1).start()
     pack_pair(0)
 
     @pl.when(ships)
@@ -234,10 +234,14 @@
             predicted = jnp.dot(uh[sl, :], wt[...], preferred_element_type=jnp.float32)
             rate = work[block, q]
             err[sl, :] = jnp.where(rate == rate, predicted - rate, 0.0).astype(jnp.bfloat16)
-        s = jnp.dot(uth[...], err[...], preferred_element_type=jnp.float32)
-        s_lo = s[0:rank, 0:128] + s[2 * rank:3 * rank, 128:256]
-        s_hi = s[rank:2 * rank, 0:128] + s[3 * rank:4 * rank, 128:256]
-        both = jnp.where(left, s_lo, s_hi)
+        both = None
+        for q in range(PIECES):
+            sl = slice(q * rows, (q + 1) * rows)
+            s = jnp.dot(uth[:, sl], err[sl, :], preferred_element_type=jnp.float32)
+            s_lo = s[0:rank, 0:128] + s[2 * rank:3 * rank, 128:256]
+            s_hi = s[rank:2 * rank, 0:128] + s[3 * rank:4 * rank, 128:256]
+            part = jnp.where(left, s_lo, s_hi)
+            both = part if both is None else both + part
         top, bottom = both[0:half], both[half:rank]
         return jnp.where(low, top, bottom) + pltpu.roll(jnp.where(low, bottom, top), 64, 1)
 
@@ -439,7 +443,7 @@
                 dma, dma((turns,)),
                 pltpu.SemaphoreType.REGULAR,
             ],
-            compiler_params=pltpu.CompilerParams(collective_id=0, has_side_effects=True, vmem_limit_bytes=67043328),
+            compiler_params=pltpu.CompilerParams(collective_id=0, has_side_effects=True, vmem_limit_bytes=53 * 1024 * 1024),
         )(ratings, mask, user_init.T, item_init.T)
         return ut.T, vt.T
 

time: 248 us -> 243 us (0.980)
  Pallas kernels: 244 us -> 239 us
    pallas_call x1, Pallas kernels: 244 us -> 239 us  [local_run(): pl.pallas_call(functools.partial(kernel, (blk_n, step_size, decay_coef)),...]
where the time goes in v5:
time: 243 us
  Pallas kernels  239 us (98%)
  local copies, waits for them, and re-layouts  2.97 us (1%)
    pallas_call x1, Pallas kernels, local_run(): pl.pallas_call(functools.partial(kernel, (blk_n, step_size, decay_coef)),...  239 us

profile of v5, /device:TPU:1, one launch (start us, length us, event | category | flops | bytes accessed | tf_op | source)
XLA Modules:
  0.0 242.7 jit_solution(12641118142678132827)
XLA Ops:
  0.6 0.0 copy-start
  0.6 0.9 copy-done
  1.6 0.0 copy-start.1
  1.6 0.7 copy-done.1
  2.3 239.1 %shard_map.59 = (f32[32,2048]{1,0:T(8,128)S(1)}, f32[32,64]{1,0:T(8,128)S(1)}) custom-call(f32[2048,512]{1,0:T(8,128)} %r_hbm.1, s32[2048,512]{1,0:T(8,128)} %m_hbm.1, f32[32,2048]{1,0:T(8,128)S(1)} %bitcast.4, f32[32,64]{1,0:T(8,128)S(1)} %bitcast.6), custom_call_target="tpu_custom_call" | custom-call | tf_op jit(solution)/shard_map/pallas_call | solution.py:410
  241.4 0.7 copy.8
  242.1 0.6 copy.9
Async XLA Ops:
  0.6 1.0 copy-start
  1.6 0.7 copy-start.1

commit v6 on v5

--- a/solution.py
+++ b/solution.py
@@ -15,10 +15,11 @@
 GROUPS = 4
 TEAM = 4
 PIECES = 4
+SPLIT = (3, 3, 1, 1)
 MESH = pl.DeviceIdType.MESH
 
 
-def kernel(dims, r_hbm, m_hbm, u_hbm, v_hbm, ut_out, vt_out, rbuf, mbuf, ubuf, vbuf, packed, work, usrc, uret, vown, vret, ut, uh, uth, wt, err, vst,
+def kernel(dims, r_hbm, m_hbm, ubuf, vbuf, ut_out, vt_out, rbuf, mbuf, packed, work, usrc, uret, vown, vret, ut, uh, uth, wt, err, vst,
            xsend, slots, xslots, vslots, load_sem, ship_send, ship_recv, user_send, user_recv, item_send, item_recv, back_send, back_recv,
            final_send, final_recv, send_sem, recv_sem, xsend_sem, xrecv_sem, vsend_sem, vrecv_sem, credit):
     blk_n, step_size, decay_coef = dims
@@ -63,10 +64,6 @@
         col = pl.multiple_of(((x + q) % pairs) * 128, 128)
         return pltpu.make_async_copy(src.at[:, pl.ds(col, 128)], dst.at[q], load_sem.at[kind, q])
 
-    load_users = pltpu.make_async_copy(u_hbm, ubuf, load_sem.at[2, 0])
-    load_items = pltpu.make_async_copy(v_hbm, vbuf, load_sem.at[2, 1])
-    load_users.start()
-    load_items.start()
     load(0, r_hbm, rbuf, 0).start()
     load(0, m_hbm, mbuf, 1).start()
 
@@ -97,10 +94,8 @@
     low = lax.broadcasted_iota(jnp.int32, (half, 128), 1) < 64
     left = lax.broadcasted_iota(jnp.int32, (rank, 128), 1) < 64
 
-    load_users.wait()
     for g in range(GROUPS):
         usrc[g * rank:(g + 1) * rank, :] = ubuf[:, g * rows:(g + 1) * rows]
-    load_items.wait()
     vown[:, 0:64] = vbuf[0:half, :]
     vown[:, 64:128] = vbuf[half:rank, :]
 
@@ -235,8 +230,10 @@
             rate = work[block, q]
             err[sl, :] = jnp.where(rate == rate, predicted - rate, 0.0).astype(jnp.bfloat16)
         both = None
-        for q in range(PIECES):
-            sl = slice(q * rows, (q + 1) * rows)
+        start = 0
+        for share in SPLIT:
+            sl = slice(start, start + share * PIECES * rows // sum(SPLIT))
+            start = sl.stop
             s = jnp.dot(uth[:, sl], err[sl, :], preferred_element_type=jnp.float32)
             s_lo = s[0:rank, 0:128] + s[2 * rank:3 * rank, 128:256]
             s_hi = s[rank:2 * rank, 0:128] + s[3 * rank:4 * rank, 128:256]
@@ -252,9 +249,8 @@
             ut[q] = old - step_size * (grad + decay_coef * old)
             halves(q)
 
-    def item_step(parts):
+    def item_step(old, parts):
         total = (parts[0] + parts[1]) + (parts[2] + parts[3])
-        old = vst[...]
         return old - step_size * (total + decay_coef * old)
 
     def await_pieces(buf, sem):
@@ -275,7 +271,7 @@
         return pltpu.make_async_remote_copy(
             src_ref=vst, dst_ref=vret, send_sem=final_send.at[q], recv_sem=final_recv, device_id=source(q), device_id_type=MESH)
 
-    def sub_epoch(t, carry):
+    def sub_epoch(t, vp):
         block = (job + t) % blk_n
 
         @pl.when(t < blk_n)
@@ -292,7 +288,7 @@
             ship(t + 2).start()
 
         for step in range(STEPS - 1):
-            spread(vst[...])
+            spread(vp)
             slots[step, place] = partial(block)
             for d in (3, 2, 1):
                 pltpu.make_async_remote_copy(
@@ -302,12 +298,13 @@
             others = slots.at[step, pl.ds(0, TEAM - 1)]
             pltpu.make_async_copy(others, others, send_sem.at[step]).wait()
             pltpu.make_async_copy(others, others, recv_sem.at[step]).wait()
-            vst[...] = item_step(slots[step])
+            vp = item_step(vp, slots[step])
+        vst[...] = vp
         ahead = pltpu.make_async_remote_copy(
             src_ref=vst, dst_ref=vslots.at[t], send_sem=vsend_sem, recv_sem=vrecv_sem.at[t],
             device_id=worker(prev_job, place), device_id_type=MESH)
         ahead.start()
-        spread(vst[...])
+        spread(vp)
         xsend[...] = partial(block)
         for d in (3, 2, 1, 0):
             pltpu.make_async_remote_copy(
@@ -328,9 +325,7 @@
         pltpu.make_async_copy(everyone, everyone, xsend_sem).wait()
         ahead.wait()
         pltpu.make_async_copy(everyone, everyone, xrecv_sem.at[t]).wait()
-        vst[...] = vslots[t]
-        vst[...] = item_step(xslots[t])
-        return carry
+        return item_step(vslots[t], xslots[t])
 
     @pl.when(is_worker)
     def _():
@@ -343,7 +338,7 @@
 
         for q in range(PIECES):
             halves(q)
-        lax.fori_loop(0, EPOCHS * blk_n, sub_epoch, 0)
+        vst[...] = lax.fori_loop(0, EPOCHS * blk_n, sub_epoch, vst[...])
         for q in (3, 2, 1):
             give_items(q).start()
 
@@ -410,13 +405,11 @@
         ut, vt = pl.pallas_call(
             functools.partial(kernel, (blk_n, step_size, decay_coef)),
             out_shape=(jax.ShapeDtypeStruct((rank, users), jnp.float32), jax.ShapeDtypeStruct((rank, items), jnp.float32)),
-            in_specs=[pl.BlockSpec(memory_space=pl.ANY)] * 4,
+            in_specs=[pl.BlockSpec(memory_space=pl.ANY)] * 2 + [vmem] * 2,
             out_specs=(vmem, vmem),
             scratch_shapes=[
                 pltpu.VMEM((blk_n // 2, users, 128), jnp.float32),
                 pltpu.VMEM((blk_n // 2, users, 128), jnp.int32),
-                pltpu.VMEM((rank, users), jnp.float32),
-                pltpu.VMEM((rank, items), jnp.float32),
                 pltpu.VMEM((blk_n, rows, wide_i), jnp.float32),
                 pltpu.VMEM((blk_n, PIECES, rows, wide_i), jnp.float32),
                 pltpu.VMEM((wide_u, rows), jnp.float32),
@@ -433,7 +426,7 @@
                 pltpu.VMEM((STEPS - 1, TEAM, half, 128), jnp.float32),
                 pltpu.VMEM((turns, TEAM, half, 128), jnp.float32),
                 pltpu.VMEM((turns, half, 128), jnp.float32),
-                dma((3, blk_n // 2)),
+                dma((2, blk_n // 2)),
                 dma((blk_n,)), dma((blk_n,)),
                 dma, dma, dma, dma,
                 dma((PIECES,)), dma,

time: 243 us -> 241 us (level)
  no operation moved by 1% of the time
where the time goes in v6:
time: 241 us
  Pallas kernels  237 us (98%)
  local copies, waits for them, and re-layouts  2.97 us (1%)
    pallas_call x1, Pallas kernels, local_run(): pl.pallas_call(functools.partial(kernel, (blk_n, step_size, decay_coef)),...  237 us

profile of v6, /device:TPU:1, one launch (start us, length us, event | category | flops | bytes accessed | tf_op | source)
XLA Modules:
  0.0 240.8 jit_solution(8421613075436118705)
XLA Ops:
  0.6 0.0 copy-start
  0.6 0.9 copy-done
  1.6 0.0 copy-start.1
  1.6 0.7 copy-done.1
  2.3 237.2 %shard_map.59 = (f32[32,2048]{1,0:T(8,128)S(1)}, f32[32,64]{1,0:T(8,128)S(1)}) custom-call(f32[2048,512]{1,0:T(8,128)} %r_hbm.1, s32[2048,512]{1,0:T(8,128)} %m_hbm.1, f32[32,2048]{1,0:T(8,128)S(1)} %bitcast.4, f32[32,64]{1,0:T(8,128)S(1)} %bitcast.6), custom_call_target="tpu_custom_call" | custom-call | tf_op jit(solution)/shard_map/pallas_call | solution.py:405
  239.5 0.7 copy.8
  240.2 0.6 copy.9
Async XLA Ops:
  0.6 1.0 copy-start
  1.6 0.7 copy-start.1

commit v7 on v6

--- a/solution.py
+++ b/solution.py
@@ -15,11 +15,11 @@
 GROUPS = 4
 TEAM = 4
 PIECES = 4
-SPLIT = (3, 3, 1, 1)
+SPLIT = (3, 3, 2)
 MESH = pl.DeviceIdType.MESH
 
 
-def kernel(dims, r_hbm, m_hbm, ubuf, vbuf, ut_out, vt_out, rbuf, mbuf, packed, work, usrc, uret, vown, vret, ut, uh, uth, wt, err, vst,
+def kernel(dims, r_hbm, m_hbm, u_hbm, v_hbm, ut_out, vt_out, rbuf, mbuf, ubuf, vbuf, packed, work, usrc, uret, vown, vret, ut, uh, uth, wt, err, vst,
            xsend, slots, xslots, vslots, load_sem, ship_send, ship_recv, user_send, user_recv, item_send, item_recv, back_send, back_recv,
            final_send, final_recv, send_sem, recv_sem, xsend_sem, xrecv_sem, vsend_sem, vrecv_sem, credit):
     blk_n, step_size, decay_coef = dims
@@ -64,6 +64,10 @@
         col = pl.multiple_of(((x + q) % pairs) * 128, 128)
         return pltpu.make_async_copy(src.at[:, pl.ds(col, 128)], dst.at[q], load_sem.at[kind, q])
 
+    load_users = pltpu.make_async_copy(u_hbm, ubuf, load_sem.at[2, 0])
+    load_items = pltpu.make_async_copy(v_hbm, vbuf, load_sem.at[2, 1])
+    load_users.start()
+    load_items.start()
     load(0, r_hbm, rbuf, 0).start()
     load(0, m_hbm, mbuf, 1).start()
 
@@ -94,8 +98,10 @@
     low = lax.broadcasted_iota(jnp.int32, (half, 128), 1) < 64
     left = lax.broadcasted_iota(jnp.int32, (rank, 128), 1) < 64
 
+    load_users.wait()
     for g in range(GROUPS):
         usrc[g * rank:(g + 1) * rank, :] = ubuf[:, g * rows:(g + 1) * rows]
+    load_items.wait()
     vown[:, 0:64] = vbuf[0:half, :]
     vown[:, 64:128] = vbuf[half:rank, :]
 
@@ -405,11 +411,13 @@
         ut, vt = pl.pallas_call(
             functools.partial(kernel, (blk_n, step_size, decay_coef)),
             out_shape=(jax.ShapeDtypeStruct((rank, users), jnp.float32), jax.ShapeDtypeStruct((rank, items), jnp.float32)),
-            in_specs=[pl.BlockSpec(memory_space=pl.ANY)] * 2 + [vmem] * 2,
+            in_specs=[pl.BlockSpec(memory_space=pl.ANY)] * 4,
             out_specs=(vmem, vmem),
             scratch_shapes=[
                 pltpu.VMEM((blk_n // 2, users, 128), jnp.float32),
                 pltpu.VMEM((blk_n // 2, users, 128), jnp.int32),
+                pltpu.VMEM((rank, users), jnp.float32),
+                pltpu.VMEM((rank, items), jnp.float32),
                 pltpu.VMEM((blk_n, rows, wide_i), jnp.float32),
                 pltpu.VMEM((blk_n, PIECES, rows, wide_i), jnp.float32),
                 pltpu.VMEM((wide_u, rows), jnp.float32),
@@ -426,7 +434,7 @@
                 pltpu.VMEM((STEPS - 1, TEAM, half, 128), jnp.float32),
                 pltpu.VMEM((turns, TEAM, half, 128), jnp.float32),
                 pltpu.VMEM((turns, half, 128), jnp.float32),
-                dma((2, blk_n // 2)),
+                dma((3, blk_n // 2)),
                 dma((blk_n,)), dma((blk_n,)),
                 dma, dma, dma, dma,
                 dma((PIECES,)), dma,
@@ -437,7 +445,7 @@
                 pltpu.SemaphoreType.REGULAR,
             ],
             compiler_params=pltpu.CompilerParams(collective_id=0, has_side_effects=True, vmem_limit_bytes=53 * 1024 * 1024),
-        )(ratings, mask, user_init.T, item_init.T)
+        )(ratings, mask, pltpu.with_memory_space_constraint(user_init.T, pltpu.HBM), pltpu.with_memory_space_constraint(item_init.T, pltpu.HBM))
         return ut.T, vt.T
 
     return jax.shard_map(local_run, mesh=mesh, in_specs=(row_spec, row_spec, row_spec, item_spec), out_specs=(row_spec, item_spec), check_vma=False)

time: 241 us -> 240 us (level)
  no operation moved by 1% of the time
where the time goes in v7:
time: 240 us
  Pallas kernels  238 us (99%)
    pallas_call x1, Pallas kernels, local_run(): pl.pallas_call(functools.partial(kernel, (blk_n, step_size, decay_coef)),...  238 us

profile of v7, /device:TPU:1, one launch (start us, length us, event | category | flops | bytes accessed | tf_op | source)
XLA Modules:
  0.0 239.7 jit_solution(5543637268181273796)
XLA Ops:
  0.6 237.7 %shard_map.59 = (f32[32,2048]{1,0:T(8,128)S(1)}, f32[32,64]{1,0:T(8,128)S(1)}) custom-call(f32[2048,512]{1,0:T(8,128)} %r_hbm.1, s32[2048,512]{1,0:T(8,128)} %m_hbm.1, f32[32,2048]{1,0:T(8,128)} %bitcast.6, f32[32,64]{1,0:T(8,128)} %bitcast.7), custom_call_target="tpu_custom_call" | custom-call | tf_op jit(solution)/shard_map/pallas_call | solution.py:411
  238.3 0.7 copy.8
  239.1 0.6 copy.9

commit v8 on v7

--- a/solution.py
+++ b/solution.py
@@ -284,15 +284,6 @@
         def _():
             await_pieces(work.at[block], ship_recv.at[block])
 
-        @pl.when(t < blk_n - 1)
-        def _():
-            pl.semaphore_signal(credit, inc=1, device_id=source(3), device_id_type=MESH)
-
-        @pl.when(jnp.logical_and(ships, t < blk_n - 2))
-        def _():
-            ship(t).wait_send()
-            ship(t + 2).start()
-
         for step in range(STEPS - 1):
             spread(vp)
             slots[step, place] = partial(block)
@@ -300,6 +291,16 @@
                 pltpu.make_async_remote_copy(
                     src_ref=slots.at[step, place], dst_ref=slots.at[step, place], send_sem=send_sem.at[step], recv_sem=recv_sem.at[step],
                     device_id=worker(job, mate(d)), device_id_type=MESH).start()
+            if step == 0:
+                @pl.when(t < blk_n - 1)
+                def _():
+                    pl.semaphore_signal(credit, inc=1, device_id=source(3), device_id_type=MESH)
+
+                @pl.when(jnp.logical_and(ships, t < blk_n - 2))
+                def _():
+                    ship(t).wait_send()
+                    ship(t + 2).start()
+
             user_step()
             others = slots.at[step, pl.ds(0, TEAM - 1)]
             pltpu.make_async_copy(others, others, send_sem.at[step]).wait()

time: 240 us -> 238 us (level)
  no operation moved by 1% of the time
where the time goes in v8:
time: 238 us
  Pallas kernels  236 us (99%)
    pallas_call x1, Pallas kernels, local_run(): pl.pallas_call(functools.partial(kernel, (blk_n, step_size, decay_coef)),...  236 us

profile of v8, /device:TPU:1, one launch (start us, length us, event | category | flops | bytes accessed | tf_op | source)
XLA Modules:
  0.0 237.9 jit_solution(16532451612042697787)
XLA Ops:
  0.6 235.9 %shard_map.59 = (f32[32,2048]{1,0:T(8,128)S(1)}, f32[32,64]{1,0:T(8,128)S(1)}) custom-call(f32[2048,512]{1,0:T(8,128)} %r_hbm.1, s32[2048,512]{1,0:T(8,128)} %m_hbm.1, f32[32,2048]{1,0:T(8,128)} %bitcast.6, f32[32,64]{1,0:T(8,128)} %bitcast.7), custom_call_target="tpu_custom_call" | custom-call | tf_op jit(solution)/shard_map/pallas_call | solution.py:412
  236.6 0.7 copy.8
  237.3 0.6 copy.9

commit v9 on v8

--- a/solution.py
+++ b/solution.py
@@ -306,12 +306,12 @@
             pltpu.make_async_copy(others, others, send_sem.at[step]).wait()
             pltpu.make_async_copy(others, others, recv_sem.at[step]).wait()
             vp = item_step(vp, slots[step])
+        spread(vp)
         vst[...] = vp
         ahead = pltpu.make_async_remote_copy(
             src_ref=vst, dst_ref=vslots.at[t], send_sem=vsend_sem, recv_sem=vrecv_sem.at[t],
             device_id=worker(prev_job, place), device_id_type=MESH)
         ahead.start()
-        spread(vp)
         xsend[...] = partial(block)
         for d in (3, 2, 1, 0):
             pltpu.make_async_remote_copy(

time: 238 us -> 238 us (level)
  no operation moved by 1% of the time
where the time goes in v9:
time: 238 us
  Pallas kernels  236 us (99%)
    pallas_call x1, Pallas kernels, local_run(): pl.pallas_call(functools.partial(kernel, (blk_n, step_size, decay_coef)),...  236 us

profile of v9, /device:TPU:1, one launch (start us, length us, event | category | flops | bytes accessed | tf_op | source)
XLA Modules:
  0.0 237.9 jit_solution(8640094098778374639)
XLA Ops:
  0.6 235.9 %shard_map.59 = (f32[32,2048]{1,0:T(8,128)S(1)}, f32[32,64]{1,0:T(8,128)S(1)}) custom-call(f32[2048,512]{1,0:T(8,128)} %r_hbm.1, s32[2048,512]{1,0:T(8,128)} %m_hbm.1, f32[32,2048]{1,0:T(8,128)} %bitcast.6, f32[32,64]{1,0:T(8,128)} %bitcast.7), custom_call_target="tpu_custom_call" | custom-call | tf_op jit(solution)/shard_map/pallas_call | solution.py:412
  236.6 0.7 copy.8
  237.3 0.6 copy.9
